TPU v7x, 32 devices: a whole 2x2x4 slice. The times are simulated.
32 devices in a mesh: tx: 4 (over x, core), ty: 4 (over z), src: 2 (over y).
Axes of the slice: x: 2, y: 2, z: 4, core: 2. Of those that a mesh axis runs over, the one named last changes fastest.
Arguments:
- spectrum: bfloat16 [2, 512, 512], P(None, ('tx', 'ty'), 'src'), may hold values from -0.0234375 to 0.0234375
- pupil_mask: int32 [256, 256], replicated, may hold values 0 or 1
- source_shifts: int32 [64, 2], P('src'), may hold values from 0 to 256
- source_weights: int32 [64], P('src'), may hold values from 0 to 8, as said below
Outputs:
- acid_level: float32 [2048, 1024], P(('tx', 'src'), 'ty')
Inputs may be any that keep to these rules, and one draw needn't show every extreme that they name: `source_weights`: the 32 consecutive sources of each group (one index of src) hold at least 4 points with weight above 0; some group has all 32 points on.
All inputs are finite; a program needn't handle non-finite values.
Results may differ from a plain program's by a relative error of at most 0.0017.
Values may be sent and summed in bfloat16 or wider, within the bound.
A program may use at most 64 MiB of HBM per device.

v0:
```python
import functools

import jax
import jax.numpy as jnp
from jax import lax
from jax.experimental import pallas as pl
from jax.experimental.pallas import tpu as pltpu
from jax.sharding import PartitionSpec as P

FRAME = 2048
BY = 256
LANES = 128
GROUP = 2
MESH = pl.DeviceIdType.MESH

diffusion_rate = 0.2


def half_angle(odd, positions):
    turns = (odd * positions) % (2 * FRAME)
    return turns.astype(jnp.float32) * (jnp.pi / FRAME)


def tables(row_count, col_count, half):
    row_block = lax.axis_index("tx") * lax.axis_size("src") + lax.axis_index("src")
    odd = 2 * jnp.arange(half, dtype=jnp.int32) + 1
    rows = row_block * row_count + jnp.arange(row_count, dtype=jnp.int32)
    cols = lax.axis_index("ty") * col_count + jnp.arange(col_count, dtype=jnp.int32)
    row_angle = half_angle(odd[None, :], rows[:, None])
    col_angle = half_angle(odd[:, None], cols[None, :])
    row_table = jnp.concatenate([jnp.cos(row_angle), jnp.sin(row_angle)], axis=1)
    col_table = jnp.concatenate([jnp.cos(col_angle), jnp.sin(col_angle)], axis=0)
    return row_table.astype(jnp.bfloat16), col_table.astype(jnp.bfloat16)


def dot(a, b):
    return jnp.dot(a, b, preferred_element_type=jnp.float32)


def reversal(size):
    rows = lax.broadcasted_iota(jnp.int32, (size, size), 0)
    cols = lax.broadcasted_iota(jnp.int32, (size, size), 1)
    return jnp.where(rows + cols == size - 1, 1.0, 0.0).astype(jnp.bfloat16)


def image_kernel(
    shifts, weights, spec_ref, pupil_ref, row_ref, col_ref, out_ref, flips, masks, acc, live, live_weight
):
    source_count = weights.shape[0]
    mask_width = spec_ref.shape[1]
    half = pupil_ref.shape[0] // 2
    tiles = mask_width // LANES
    block = 256

    turn = reversal(block)
    for plane in range(2):
        for i in range(mask_width // block):
            for j in range(mask_width // block):
                ri, rj = mask_width // block - 1 - i, mask_width // block - 1 - j
                cell = spec_ref[plane, block * i : block * (i + 1), block * j : block * (j + 1)]
                col_flip = dot(cell, turn)
                row_flip = dot(turn, cell)
                both = dot(turn, col_flip.astype(jnp.bfloat16))
                for version, value, vi, vj in (
                    (0, cell.astype(jnp.float32), i, j),
                    (1, row_flip, ri, j),
                    (2, col_flip, i, rj),
                    (3, both, ri, rj),
                ):
                    for t in range(block // LANES):
                        slot = (version * 2 + plane) * tiles + vj * (block // LANES) + t
                        flips[slot, block * vi : block * (vi + 1), :] = value[:, LANES * t : LANES * (t + 1)]
    small = reversal(half)
    pupil = pupil_ref[...].astype(jnp.float32).astype(jnp.bfloat16)
    masks[0] = pupil[half:, half:].astype(jnp.float32)
    masks[1] = dot(small, pupil[:half, half:])
    masks[2] = dot(pupil[half:, :half], small)
    masks[3] = dot(small, dot(pupil[:half, :half], small).astype(jnp.bfloat16))

    def clear(i, carry):
        live[i] = 0
        live_weight[i] = 0
        return carry

    lax.fori_loop(0, source_count + GROUP, clear, 0)

    def pick(i, count):
        weight = weights[i]
        live[count] = i
        live_weight[count] = jnp.maximum(weight, 0)
        return count + (weight > 0).astype(jnp.int32)

    count = lax.fori_loop(0, source_count, pick, jnp.int32(0))
    live_weight[count] = 0

    acc[...] = jnp.zeros_like(acc)
    lane = lax.broadcasted_iota(jnp.int32, (half, LANES), 1)

    def fold(a, b):
        row_offsets = (a + half, mask_width - half - a)
        col_offsets = (b + half, mask_width - half - b)
        parts = []
        for plane in range(2):
            quads = []
            for col_side in range(2):
                off = col_offsets[col_side]
                tile, rest = off // LANES, off % LANES
                after = jnp.minimum(tile + 1, tiles - 1)
                back = (LANES - rest) % LANES
                for row_side in range(2):
                    version = 2 * col_side + row_side
                    base = (version * 2 + plane) * tiles
                    rows = pl.ds(row_offsets[row_side], half)
                    left = flips[base + tile, rows, :]
                    right = flips[base + after, rows, :]
                    merged = jnp.where(lane >= rest, left, right)
                    quads.append(pltpu.roll(merged, back, 1) * masks[version])
            s1, d1 = quads[0] + quads[1], quads[0] - quads[1]
            s2, d2 = quads[2] + quads[3], quads[2] - quads[3]
            parts.append((s1, d1, s2, d2))
        (s1, d1, s2, d2), (t1, e1, t2, e2) = parts
        return (
            jnp.concatenate([s1 + s2, t2 - t1], axis=1),
            jnp.concatenate([-(e1 + e2), d2 - d1], axis=1),
            jnp.concatenate([t1 + t2, s1 - s2], axis=1),
            jnp.concatenate([d1 + d2, e2 - e1], axis=1),
        )

    def turn_body(step, carry):
        total = jnp.zeros(acc.shape, jnp.float32)
        for g in range(GROUP):
            index = step * GROUP + g
            source = live[index]
            weight = live_weight[index].astype(jnp.float32)
            folded = jnp.concatenate(fold(shifts[source, 0], shifts[source, 1]), axis=0).astype(jnp.bfloat16)
            inner = dot(folded, col_ref[...]).astype(jnp.bfloat16)
            real = dot(row_ref[...], inner[: 2 * half])
            imag = dot(row_ref[...], inner[2 * half :])
            total = total + weight * (real * real + imag * imag)
        acc[...] += total
        return carry

    lax.fori_loop(0, (count + GROUP - 1) // GROUP, turn_body, 0)
    out_ref[...] = 1.0 - jnp.exp(-(acc[...] / (2.0 * source_count)))


def image(shifts, weights, spectrum, pupil_mask, row_table, col_table):
    source_count = weights.shape[0]
    mask_width = spectrum.shape[1]
    half = pupil_mask.shape[0] // 2
    tile = (row_table.shape[0], col_table.shape[1])
    smem = pl.BlockSpec(memory_space=pltpu.SMEM)
    vmem = pl.BlockSpec(memory_space=pltpu.VMEM)
    return pl.pallas_call(
        image_kernel,
        out_shape=jax.ShapeDtypeStruct(tile, jnp.float32),
        in_specs=[smem, smem, vmem, vmem, vmem, vmem],
        out_specs=vmem,
        scratch_shapes=[
            pltpu.VMEM((8 * mask_width // LANES, mask_width, LANES), jnp.float32),
            pltpu.VMEM((4, half, half), jnp.float32),
            pltpu.VMEM(tile, jnp.float32),
            pltpu.SMEM((source_count + GROUP,), jnp.int32),
            pltpu.SMEM((source_count + GROUP,), jnp.int32),
        ],
        name="image",
    )(shifts, weights, spectrum, pupil_mask, row_table, col_table)


def diffuse_kernel(sizes, acid_ref, out_ref, strips, corners, edges, beside, send_sem, recv_sem):
    tx_count, ty_count, src_count = sizes
    rows, cols = acid_ref.shape
    row_block = lax.axis_index("tx") * src_count + lax.axis_index("src")
    col_block = lax.axis_index("ty")
    row_blocks = tx_count * src_count

    def device(dr, dc):
        other = lax.rem(row_block + row_blocks + dr, row_blocks)
        return {
            "tx": other // src_count,
            "src": lax.rem(other, src_count),
            "ty": lax.rem(col_block + ty_count + dc, ty_count),
        }

    around = [(dr, dc) for dr in (-1, 0, 1) for dc in (-1, 0, 1) if (dr, dc) != (0, 0)]
    barrier = pltpu.get_barrier_semaphore()
    for dr, dc in around:
        pl.semaphore_signal(barrier, inc=1, device_id=device(dr, dc), device_id_type=MESH)
    strips[0] = acid_ref[:, :LANES].T[:8]
    strips[1] = acid_ref[:, cols - LANES :].T[LANES - 8 :]
    pl.semaphore_wait(barrier, len(around))

    copies = []
    for n, (dr, dc) in enumerate(around):
        if dc == 0:
            src = acid_ref.at[:8] if dr < 0 else acid_ref.at[rows - 8 :]
            dst = edges.at[0 if dr > 0 else 1]
        elif dr == 0:
            src = strips.at[0 if dc < 0 else 1]
            dst = beside.at[0 if dc > 0 else 1]
        else:
            row_part = slice(0, 8) if dr < 0 else slice(rows - 8, rows)
            col_part = slice(0, LANES) if dc < 0 else slice(cols - LANES, cols)
            src = acid_ref.at[row_part, col_part]
            dst = corners.at[(0 if dr > 0 else 2) + (0 if dc > 0 else 1)]
        copy = pltpu.make_async_remote_copy(
            src_ref=src,
            dst_ref=dst,
            send_sem=send_sem.at[n],
            recv_sem=recv_sem.at[n],
            device_id=device(dr, dc),
            device_id_type=MESH,
        )
        copy.start()
        copies.append(copy)
    for copy in copies:
        copy.wait()

    none = jnp.zeros((LANES - 8, rows), jnp.float32)
    left = jnp.concatenate([none, beside[0]], axis=0).T
    right = jnp.concatenate([beside[1], none], axis=0).T
    level = jnp.concatenate(
        [
            jnp.concatenate([corners[0], edges[0], corners[1]], axis=1),
            jnp.concatenate([left, acid_ref[...], right], axis=1),
            jnp.concatenate([corners[2], edges[1], corners[3]], axis=1),
        ],
        axis=0,
    )
    x = row_block * rows - 8 + lax.broadcasted_iota(jnp.int32, level.shape, 0)
    y = col_block * cols - LANES + lax.broadcasted_iota(jnp.int32, level.shape, 1)
    inside = (x >= 0) & (x < row_blocks * rows) & (y >= 0) & (y < ty_count * cols)
    tall, wide = level.shape
    for repeat in range(2):
        level = jnp.where(inside, level, 0.0)
        near = (
            pltpu.roll(level, 1, 0)
            + pltpu.roll(level, tall - 1, 0)
            + pltpu.roll(level, 1, 1)
            + pltpu.roll(level, wide - 1, 1)
        )
        level = level + diffusion_rate * (near - 4.0 * level)
    out_ref[...] = level[8 : 8 + rows, LANES : LANES + cols]


def diffuse(acid, sizes):
    rows, cols = acid.shape
    vmem = pl.BlockSpec(memory_space=pltpu.VMEM)
    return pl.pallas_call(
        functools.partial(diffuse_kernel, sizes),
        out_shape=jax.ShapeDtypeStruct((rows, cols), jnp.float32),
        in_specs=[vmem],
        out_specs=vmem,
        scratch_shapes=[
            pltpu.VMEM((2, 8, rows), jnp.float32),
            pltpu.VMEM((4, 8, LANES), jnp.float32),
            pltpu.VMEM((2, 8, cols), jnp.float32),
            pltpu.VMEM((2, 8, rows), jnp.float32),
            pltpu.SemaphoreType.DMA((8,)),
            pltpu.SemaphoreType.DMA((8,)),
        ],
        compiler_params=pltpu.CompilerParams(collective_id=1, has_side_effects=True),
        name="diffuse",
    )(acid)


def body(sizes, spectrum, pupil_mask, source_shifts, source_weights):
    partial_spec = lax.all_gather(spectrum, "src", axis=2, tiled=True)
    spectrum_all = lax.all_gather(partial_spec, ("tx", "ty"), axis=1, tiled=True)
    shifts = lax.all_gather(source_shifts, "src", axis=0, tiled=True)
    weights = lax.all_gather(source_weights, "src", axis=0, tiled=True)
    tx_count, ty_count, src_count = sizes
    rows = FRAME // (tx_count * src_count)
    row_table, col_table = tables(rows, BY, pupil_mask.shape[0] // 2)
    acid = image(shifts, weights, spectrum_all, pupil_mask, row_table, col_table)
    return diffuse(acid, sizes)


def solution(mesh):
    sizes = (mesh.shape["tx"], mesh.shape["ty"], mesh.shape["src"])
    placed = (P(None, ("tx", "ty"), "src"), P(), P("src", None), P("src"))
    return jax.shard_map(
        functools.partial(body, sizes),
        mesh=mesh,
        in_specs=placed,
        out_specs=P(("tx", "src"), "ty"),
        check_vma=False,
    )
```

profile of v0, /device:TPU:0, one launch (start us, length us, event | category | flops | bytes accessed | tf_op | source)
XLA Modules:
  0.0 93.7 jit_solution(16182712306694913760)
XLA Ops:
  6.5 0.0 all-gather.3.cloned.1.call-start
  6.5 7.2 %all_gather.14 = bf16[2,32,512]{2,1,0:T(8,128)(2,1)} all-gather(bf16[2,32,256]{2,1,0:T(8,128)(2,1)} %param.4), channel_id=1, replica_groups=mesh['tx'=4,'ty'=4,'src'=2] {'src'}, dimensions={2}, use_global_device_ids=true | all-gather | bytes 98304 | tf_op jit(solution)/shard_map/all_gather | solution.py:268
  13.7 0.0 all-gather.3.cloned.1.call-update
  13.8 0.0 copy-start
  13.8 0.7 copy-done
  14.5 4.2 %all-gather = s32[2,32,2]{1,2,0:T(2,128)S(1)} all-gather(s32[1,32,2]{1,2,0:T(2,128)S(1)} %bitcast.4), channel_id=1, replica_groups=mesh['tx'=4,'ty'=4,'src'=2] {'src'}, dimensions={0}, use_global_device_ids=true | all-gather | bytes 768 | tf_op jit(solution)/shard_map/all_gather | solution.py:270
  18.7 0.0 copy-start.2
  18.7 0.7 copy.9
  19.4 0.0 copy-done.2
  19.4 0.6 dynamic-slice
  20.6 0.0 copy-start.1
  20.7 0.6 copy-done.1
  21.3 0.2 dynamic-update-slice
  21.5 4.8 %all-reduce.weights = s32[64]{0:T(128)} all-reduce(s32[64]{0:T(128)S(1)} %dynamic-update-slice), channel_id=1, replica_groups=mesh['tx'=4,'ty'=4,'src'=2] {'src'}, use_global_device_ids=true, to_apply=%add | all-reduce | flops 64 | bytes 512
  26.3 0.6 cosine_convert_fusion.1
  26.9 0.6 cosine_convert_fusion
  27.5 0.7 pad_maximum_fusion
  28.2 24.0 %all-gather.3.cloned.1.call-done.spec_ref = bf16[2,512,512]{2,1,0:T(8,128)(2,1)} async-done(((bf16[2,32,512]{2,1,0:T(8,128)(2,1)}), bf16[2,512,512]{2,1,0:T(8,128)(2,1)}) %all-gather.3.cloned.1.call-update) | async-done | bytes 1048592 | tf_op jit(solution)/shard_map/all_gather | solution.py:269
  52.3 23.4 %image.1.acid_ref = f32[256,256]{1,0:T(8,128)} custom-call(s32[64,2]{1,0:T(8,128)} %bitcast.3, s32[64]{0:T(128)} %all-reduce.weights, bf16[2,512,512]{2,1,0:T(8,128)(2,1)} %all-gather.3.cloned.1.call-done.spec_ref, s32[256,256]{1,0:T(8,128)} %pupil_ref.1, bf16[256,256]{1,0:T(8,128)(2,1)} %get-tuple-element.9.row_ref, bf16[256,256]{1,0:T(8,128)(2,1)} %get-tuple-element.10.col_ref), custom_call_target="tpu_custom_call" | custom-call | tf_op jit(solution)/shard_map/image/pallas_call | solution.py:154
  75.6 9.5 %diffuse.1 = f32[256,256]{1,0:T(8,128)} custom-call(f32[256,256]{1,0:T(8,128)} %image.1.acid_ref), custom_call_target="tpu_custom_call" | custom-call | tf_op jit(solution)/shard_map/diffuse/pallas_call | solution.py:249
  85.2 1.7 %copy.13 = f32[256,256]{1,0:T(8,128)} copy(f32[256,256]{1,0:T(8,128)} %diffuse.1) | data formatting | bytes 524288
  (4 shorter events, 0.0 us)
Async XLA Ops:
  6.5 45.7 %all-gather.3.cloned.1.call-start = ((), (), s32[]{:S(2)}) async-start(), calls=%async_computation | async-start | bytes 1114112 | tf_op jit(solution)/shard_map/all_gather | solution.py:269
  13.8 0.7 copy-start
  18.7 0.7 copy-start.2
  20.6 0.7 copy-start.1
Sparse Core Ops, SparseCore 0:
  13.9 38.3 all-gather.2
where the time goes:
time: 92 us; the launch traced here: 93.7 us
  Pallas kernels  32.9 us (36%)
  waiting for transfers between devices  24 us (26%)
  blocking collectives  16.2 us (18%)
  between operations  14.1 us (15%)
  local copies, waits for them, and re-layouts  4.47 us (5%)
  other arithmetic  1.94 us (2%)
    all_gather x1, waiting for transfers between devices, body(): lax.all_gather(partial_spec, ('tx', 'ty'), axis=1, tiled=True)  24 us
    pallas_call x1, Pallas kernels, image(): pl.pallas_call(image_kernel, out_shape=jax.ShapeDtypeStruct(tile, jnp.flo...  23.4 us
    pallas_call x1, Pallas kernels, diffuse(): pl.pallas_call(functools.partial(diffuse_kernel, sizes), out_shape=jax.Sh...  9.52 us
    all_gather x1, blocking collectives, body(): partial_spec = lax.all_gather(spectrum, 'src', axis=2, tiled=True)  7.21 us
    unnamed x1, blocking collectives  4.78 us
    unnamed x11, local copies, waits for them, and re-layouts  4.47 us
    all_gather x1, blocking collectives, body(): shifts = lax.all_gather(source_shifts, 'src', axis=0, tiled=True)  4.23 us
  transfers between devices with their start and end apart: 1, of which 1 were waited for; matrix products, arithmetic and copies ran while one was open for 4% of the time, Pallas kernels for 0%

commit v1 on v0

--- a/solution.py
+++ b/solution.py
@@ -17,20 +17,12 @@
 
 
 def half_angle(odd, positions):
-    turns = (odd * positions) % (2 * FRAME)
+    turns = (odd * positions) & (2 * FRAME - 1)
     return turns.astype(jnp.float32) * (jnp.pi / FRAME)
 
 
-def tables(row_count, col_count, half):
-    row_block = lax.axis_index("tx") * lax.axis_size("src") + lax.axis_index("src")
-    odd = 2 * jnp.arange(half, dtype=jnp.int32) + 1
-    rows = row_block * row_count + jnp.arange(row_count, dtype=jnp.int32)
-    cols = lax.axis_index("ty") * col_count + jnp.arange(col_count, dtype=jnp.int32)
-    row_angle = half_angle(odd[None, :], rows[:, None])
-    col_angle = half_angle(odd[:, None], cols[None, :])
-    row_table = jnp.concatenate([jnp.cos(row_angle), jnp.sin(row_angle)], axis=1)
-    col_table = jnp.concatenate([jnp.cos(col_angle), jnp.sin(col_angle)], axis=0)
-    return row_table.astype(jnp.bfloat16), col_table.astype(jnp.bfloat16)
+def iota(shape, dim):
+    return lax.broadcasted_iota(jnp.int32, shape, dim)
 
 
 def dot(a, b):
@@ -43,12 +35,204 @@
     return jnp.where(rows + cols == size - 1, 1.0, 0.0).astype(jnp.bfloat16)
 
 
+def gather_kernel(
+    sizes, spec_ref, shift_ref, weight_ref, pupil_ref, all_ref, shifts_ref, weights_ref, row_ref, col_ref, mask_ref,
+    send_sem, recv_sem, side_send, side_recv,
+):
+    tx_count, ty_count, src_count = sizes
+    pair_count = tx_count // 2
+    tx, t, s = lax.axis_index("tx"), lax.axis_index("ty"), lax.axis_index("src")
+    pair, core = tx // 2, lax.rem(tx, 2)
+    other_core = 1 - core
+    far_t = [lax.rem(t + d, ty_count) for d in range(1, ty_count)]
+    far_s = [lax.rem(s + d, src_count) for d in range(1, src_count)]
+    far_pair = [lax.rem(pair + d, pair_count) for d in range(1, pair_count)]
+
+    def along_ty(i):
+        return {"tx": tx, "ty": i, "src": s}
+
+    def along_src(i):
+        return {"tx": tx, "ty": t, "src": i}
+
+    def along_pair(i):
+        return {"tx": 2 * i + core, "ty": t, "src": s}
+
+    across = {"tx": 2 * pair + other_core, "ty": t, "src": s}
+    partners = [along_ty(i) for i in far_t] + [along_src(i) for i in far_s]
+    partners += [along_pair(i) for i in far_pair] + [across]
+    barrier = pltpu.get_barrier_semaphore()
+    for partner in partners:
+        pl.semaphore_signal(barrier, inc=1, device_id=partner, device_id_type=MESH)
+    pl.semaphore_wait(barrier, len(partners))
+
+    started = []
+
+    def send(plane, piece, device):
+        i, j, k = piece
+        slot = all_ref.at[k, plane, i, j]
+        own = i is tx and j is t and k is s
+        copy = pltpu.make_async_remote_copy(
+            src_ref=spec_ref.at[plane] if own else slot,
+            dst_ref=slot,
+            send_sem=send_sem.at[len(started)],
+            recv_sem=recv_sem.at[plane, k, i, j],
+            device_id=device,
+            device_id_type=MESH,
+        )
+        copy.start()
+        started.append(copy)
+
+    def arrive(plane, piece):
+        i, j, k = piece
+        slot = all_ref.at[k, plane, i, j]
+        pltpu.make_async_remote_copy(
+            src_ref=slot,
+            dst_ref=slot,
+            send_sem=send_sem.at[0],
+            recv_sem=recv_sem.at[plane, k, i, j],
+            device_id=across,
+            device_id_type=MESH,
+        ).wait_recv()
+
+    side = []
+    for n, i in enumerate(far_s):
+        for m, (src, dst) in enumerate(((shift_ref, shifts_ref), (weight_ref, weights_ref))):
+            copy = pltpu.make_async_remote_copy(
+                src_ref=src,
+                dst_ref=dst.at[s],
+                send_sem=side_send.at[m, n],
+                recv_sem=side_recv.at[m, s],
+                device_id=along_src(i),
+                device_id_type=MESH,
+            )
+            copy.start()
+            side.append(copy)
+
+    def spread(plane, piece):
+        for i in far_s:
+            send(plane, piece, along_src(i))
+        for i in far_pair:
+            send(plane, piece, along_pair(i))
+        send(plane, piece, across)
+
+    own = (tx, t, s)
+    for plane in range(2):
+        for i in far_t:
+            send(plane, own, along_ty(i))
+    for plane in range(2):
+        spread(plane, own)
+
+    shifts_ref[s] = shift_ref[...]
+    weights_ref[s] = weight_ref[...]
+    for plane in range(2):
+        all_ref[s, plane, tx, t] = spec_ref[plane]
+    half = pupil_ref.shape[0] // 2
+    rows, cols = row_ref.shape[0], col_ref.shape[1]
+    x = (tx * src_count + s) * rows + iota((rows, half), 0)
+    row_angle = half_angle(2 * iota((rows, half), 1) + 1, x)
+    row_ref[:, :half] = jnp.cos(row_angle).astype(jnp.bfloat16)
+    row_ref[:, half:] = jnp.sin(row_angle).astype(jnp.bfloat16)
+    y = t * cols + iota((half, cols), 1)
+    col_angle = half_angle(2 * iota((half, cols), 0) + 1, y)
+    col_ref[:half] = jnp.cos(col_angle).astype(jnp.bfloat16)
+    col_ref[half:] = jnp.sin(col_angle).astype(jnp.bfloat16)
+    small = reversal(half)
+    pupil = pupil_ref[...].astype(jnp.float32).astype(jnp.bfloat16)
+    mask_ref[0] = pupil[half:, half:].astype(jnp.float32)
+    mask_ref[1] = dot(small, pupil[:half, half:])
+    mask_ref[2] = dot(pupil[half:, :half], small)
+    mask_ref[3] = dot(small, dot(pupil[:half, :half], small).astype(jnp.bfloat16))
+
+    near_first = [t] + far_t
+    for j in far_t:
+        for plane in range(2):
+            arrive(plane, (tx, j, s))
+            spread(plane, (tx, j, s))
+    for j in near_first:
+        for k in far_s:
+            arrive(0, (tx, j, k))
+            for i in far_pair:
+                send(0, (tx, j, k), along_pair(i))
+            send(0, (tx, j, k), across)
+        for i in far_pair:
+            there = 2 * i + core
+            arrive(1, (there, j, s))
+            for k in far_s:
+                send(1, (there, j, s), along_src(k))
+            send(1, (there, j, s), across)
+        for k in far_s:
+            arrive(1, (tx, j, k))
+            send(1, (tx, j, k), across)
+        for i in far_pair:
+            arrive(0, (2 * i + core, j, s))
+            send(0, (2 * i + core, j, s), across)
+    for j in near_first:
+        for i in far_pair:
+            for k in far_s:
+                for plane in range(2):
+                    arrive(plane, (2 * i + core, j, k))
+                    send(plane, (2 * i + core, j, k), across)
+    for j in near_first:
+        for i in [pair] + far_pair:
+            for k in [s] + far_s:
+                for plane in range(2):
+                    arrive(plane, (2 * i + other_core, j, k))
+    for n, i in enumerate(far_s):
+        for m, (src, dst) in enumerate(((shift_ref, shifts_ref), (weight_ref, weights_ref))):
+            pltpu.make_async_remote_copy(
+                src_ref=src,
+                dst_ref=dst.at[i],
+                send_sem=side_send.at[m, n],
+                recv_sem=side_recv.at[m, i],
+                device_id=across,
+                device_id_type=MESH,
+            ).wait_recv()
+    for copy in started + side:
+        copy.wait_send()
+
+
+def gather(spectrum, source_shifts, source_weights, pupil_mask, sizes):
+    tx_count, ty_count, src_count = sizes
+    pair_count = tx_count // 2
+    _, block_rows, block_cols = spectrum.shape
+    slots = source_weights.shape[0]
+    half = pupil_mask.shape[0] // 2
+    rows = FRAME // (tx_count * src_count)
+    vmem = pl.BlockSpec(memory_space=pltpu.VMEM)
+    lines = pair_count * src_count * ty_count
+    sends = 2 * (ty_count - 1) + 2 * lines + 2 * ty_count * (src_count - 1 + pair_count - 1)
+    sends += 2 * ty_count * (src_count - 1) * (pair_count - 1)
+    return pl.pallas_call(
+        functools.partial(gather_kernel, sizes),
+        out_shape=(
+            jax.ShapeDtypeStruct((src_count, 2, tx_count, ty_count, block_rows, block_cols), jnp.bfloat16),
+            jax.ShapeDtypeStruct((src_count, slots, 2), jnp.int32),
+            jax.ShapeDtypeStruct((src_count, 1, slots), jnp.int32),
+            jax.ShapeDtypeStruct((rows, 2 * half), jnp.bfloat16),
+            jax.ShapeDtypeStruct((2 * half, BY), jnp.bfloat16),
+            jax.ShapeDtypeStruct((4, half, half), jnp.float32),
+        ),
+        in_specs=[vmem] * 4,
+        out_specs=(vmem,) * 6,
+        scratch_shapes=[
+            pltpu.SemaphoreType.DMA((sends,)),
+            pltpu.SemaphoreType.DMA((2, src_count, tx_count, ty_count)),
+            pltpu.SemaphoreType.DMA((2, src_count)),
+            pltpu.SemaphoreType.DMA((2, src_count)),
+        ],
+        compiler_params=pltpu.CompilerParams(collective_id=0, has_side_effects=True),
+        name="gather",
+    )(spectrum, source_shifts, source_weights[None], pupil_mask)
+
+
 def image_kernel(
-    shifts, weights, spec_ref, pupil_ref, row_ref, col_ref, out_ref, flips, masks, acc, live, live_weight
+    shifts, weights, spec_ref, masks, row_ref, col_ref, out_ref, flips, acc, live_row, live_col, live_weight
 ):
-    source_count = weights.shape[0]
-    mask_width = spec_ref.shape[1]
-    half = pupil_ref.shape[0] // 2
+    src_count, _, slots = weights.shape
+    source_count = src_count * slots
+    mask_width = spec_ref.shape[2]
+    part = spec_ref.shape[3]
+    half = masks.shape[1]
     tiles = mask_width // LANES
     block = 256
 
@@ -57,7 +241,9 @@
         for i in range(mask_width // block):
             for j in range(mask_width // block):
                 ri, rj = mask_width // block - 1 - i, mask_width // block - 1 - j
-                cell = spec_ref[plane, block * i : block * (i + 1), block * j : block * (j + 1)]
+                rows = slice(block * i, block * (i + 1))
+                cells = [spec_ref[k, plane, rows] for k in range(block * j // part, -(-block * (j + 1) // part))]
+                cell = cells[0] if len(cells) == 1 else jnp.concatenate(cells, axis=1)
                 col_flip = dot(cell, turn)
                 row_flip = dot(turn, cell)
                 both = dot(turn, col_flip.astype(jnp.bfloat16))
@@ -70,28 +256,20 @@
                     for t in range(block // LANES):
                         slot = (version * 2 + plane) * tiles + vj * (block // LANES) + t
                         flips[slot, block * vi : block * (vi + 1), :] = value[:, LANES * t : LANES * (t + 1)]
-    small = reversal(half)
-    pupil = pupil_ref[...].astype(jnp.float32).astype(jnp.bfloat16)
-    masks[0] = pupil[half:, half:].astype(jnp.float32)
-    masks[1] = dot(small, pupil[:half, half:])
-    masks[2] = dot(pupil[half:, :half], small)
-    masks[3] = dot(small, dot(pupil[:half, :half], small).astype(jnp.bfloat16))
-
-    def clear(i, carry):
-        live[i] = 0
-        live_weight[i] = 0
-        return carry
-
-    lax.fori_loop(0, source_count + GROUP, clear, 0)
 
     def pick(i, count):
-        weight = weights[i]
-        live[count] = i
-        live_weight[count] = jnp.maximum(weight, 0)
+        group, slot = i // slots, lax.rem(i, slots)
+        weight = weights[group, 0, slot]
+        live_row[count] = shifts[group, slot, 0]
+        live_col[count] = shifts[group, slot, 1]
+        live_weight[count] = weight
         return count + (weight > 0).astype(jnp.int32)
 
     count = lax.fori_loop(0, source_count, pick, jnp.int32(0))
-    live_weight[count] = 0
+    for g in range(GROUP):
+        live_row[count + g] = 0
+        live_col[count + g] = 0
+        live_weight[count + g] = 0
 
     acc[...] = jnp.zeros_like(acc)
     lane = lax.broadcasted_iota(jnp.int32, (half, LANES), 1)
@@ -130,9 +308,8 @@
         total = jnp.zeros(acc.shape, jnp.float32)
         for g in range(GROUP):
             index = step * GROUP + g
-            source = live[index]
             weight = live_weight[index].astype(jnp.float32)
-            folded = jnp.concatenate(fold(shifts[source, 0], shifts[source, 1]), axis=0).astype(jnp.bfloat16)
+            folded = jnp.concatenate(fold(live_row[index], live_col[index]), axis=0).astype(jnp.bfloat16)
             inner = dot(folded, col_ref[...]).astype(jnp.bfloat16)
             real = dot(row_ref[...], inner[: 2 * half])
             imag = dot(row_ref[...], inner[2 * half :])
@@ -144,10 +321,9 @@
     out_ref[...] = 1.0 - jnp.exp(-(acc[...] / (2.0 * source_count)))
 
 
-def image(shifts, weights, spectrum, pupil_mask, row_table, col_table):
-    source_count = weights.shape[0]
-    mask_width = spectrum.shape[1]
-    half = pupil_mask.shape[0] // 2
+def image(spectrum, shifts, weights, row_table, col_table, masks):
+    source_count = weights.shape[0] * weights.shape[2]
+    mask_width = spectrum.shape[2]
     tile = (row_table.shape[0], col_table.shape[1])
     smem = pl.BlockSpec(memory_space=pltpu.SMEM)
     vmem = pl.BlockSpec(memory_space=pltpu.VMEM)
@@ -158,13 +334,11 @@
         out_specs=vmem,
         scratch_shapes=[
             pltpu.VMEM((8 * mask_width // LANES, mask_width, LANES), jnp.float32),
-            pltpu.VMEM((4, half, half), jnp.float32),
             pltpu.VMEM(tile, jnp.float32),
-            pltpu.SMEM((source_count + GROUP,), jnp.int32),
-            pltpu.SMEM((source_count + GROUP,), jnp.int32),
-        ],
+        ]
+        + [pltpu.SMEM((source_count + GROUP,), jnp.int32)] * 3,
         name="image",
-    )(shifts, weights, spectrum, pupil_mask, row_table, col_table)
+    )(shifts, weights, spectrum, masks, row_table, col_table)
 
 
 def diffuse_kernel(sizes, acid_ref, out_ref, strips, corners, edges, beside, send_sem, recv_sem):
@@ -265,14 +439,12 @@
 
 
 def body(sizes, spectrum, pupil_mask, source_shifts, source_weights):
-    partial_spec = lax.all_gather(spectrum, "src", axis=2, tiled=True)
-    spectrum_all = lax.all_gather(partial_spec, ("tx", "ty"), axis=1, tiled=True)
-    shifts = lax.all_gather(source_shifts, "src", axis=0, tiled=True)
-    weights = lax.all_gather(source_weights, "src", axis=0, tiled=True)
-    tx_count, ty_count, src_count = sizes
-    rows = FRAME // (tx_count * src_count)
-    row_table, col_table = tables(rows, BY, pupil_mask.shape[0] // 2)
-    acid = image(shifts, weights, spectrum_all, pupil_mask, row_table, col_table)
+    pieces, shifts, weights, row_table, col_table, masks = gather(
+        spectrum, source_shifts, source_weights, pupil_mask, sizes
+    )
+    src_count, _, tx_count, ty_count, block_rows, block_cols = pieces.shape
+    columns = pieces.reshape(src_count, 2, tx_count * ty_count * block_rows, block_cols)
+    acid = image(columns, shifts, weights, row_table, col_table, masks)
     return diffuse(acid, sizes)
 
 

time: 92 us -> 55.9 us (0.61); the launches traced: 93.7 us -> 55.6 us
  waiting for transfers between devices: 24 us -> 0 us
  Pallas kernels: 32.9 us -> 52.6 us
  blocking collectives: 16.2 us -> 0 us
  between operations: 14.1 us -> 0.02 us
  other arithmetic: 1.94 us -> 0 us
  local copies, waits for them, and re-layouts: 4.47 us -> 3.04 us
    all_gather x1 -> x0, waiting for transfers between devices: 24 us -> none  [body(): lax.all_gather(partial_spec, ('tx', 'ty'), axis=1, tiled=True)]
    pallas_call x0 -> x1, Pallas kernels: none -> 19.7 us  [gather(): pl.pallas_call(functools.partial(gather_kernel, sizes), out_shape=(jax.Sh...]
    all_gather x2 -> x0, blocking collectives: 11.4 us -> none  [the longest x1 7.21 us: body(): partial_spec = lax.all_gather(spectrum, 'src', axis=2, tiled=True)]
    unnamed x1 -> x0, blocking collectives: 4.78 us -> none
    unnamed x11 -> x4, local copies, waits for them, and re-layouts: 4.47 us -> 3.04 us
    another operation x2 -> x0, other arithmetic: 1.2 us -> none
  transfers between devices with their start and end apart: 1 -> 0, of which waited for: 1 -> 0; matrix products, arithmetic and copies ran while one was open for 4% -> 0% of each run, Pallas kernels for 0% -> 0%
where the time goes in v1:
time: 55.9 us; the launch traced here: 55.6 us
  Pallas kernels  52.6 us (94%)
  local copies, waits for them, and re-layouts  3.04 us (5%)
    pallas_call x1, Pallas kernels, image(): pl.pallas_call(image_kernel, out_shape=jax.ShapeDtypeStruct(tile, jnp.flo...  23.2 us
    pallas_call x1, Pallas kernels, gather(): pl.pallas_call(functools.partial(gather_kernel, sizes), out_shape=(jax.Sh...  19.7 us
    pallas_call x1, Pallas kernels, diffuse(): pl.pallas_call(functools.partial(diffuse_kernel, sizes), out_shape=jax.Sh...  9.7 us
    unnamed x4, local copies, waits for them, and re-layouts  3.04 us

profile of v1, /device:TPU:0, one launch (start us, length us, event | category | flops | bytes accessed | tf_op | source)
XLA Modules:
  0.0 55.6 jit_solution(16704736094532803885)
XLA Ops:
  0.0 0.0 copy-start
  0.0 0.7 %copy-done = s32[32,2]{0,1:T(2,128)S(1)} copy-done((s32[32,2]{0,1:T(2,128)S(1)}, s32[32,2]{0,1:T(2,128)}, u32[]{:S(2)}) %copy-start) | copy-done | bytes 280
  0.7 0.7 %copy.5.shift_ref = s32[32,2]{1,0:T(8,128)} copy(s32[32,2]{0,1:T(2,128)S(1)} %copy-done) | data formatting | bytes 512 | tf_op args[2]
  1.4 19.7 %gather.1 = (bf16[2,2,4,4,32,256]{5,4,3,2,1,0:T(8,128)(2,1)}, s32[2,32,2]{2,1,0:T(8,128)}, s32[2,1,32]{2,1,0:T(1,128)}, bf16[256,256]{1,0:T(8,128)(2,1)}, bf16[2...) custom-call(bf16[2,32,256]{2,1,0:T(8,128)(2,1)} %spec_ref.1, s32[32,2]{1,0:T(8,128)} %copy.5.shift_ref, s32[1,32]{1,0:T(1,128)} %bitcast.3, ...), custom_call_target="tpu_custom_call" | custom-call | tf_op jit(solution)/shard_map/gather/pallas_call | solution.py:205
  21.1 23.2 %image.1.acid_ref = f32[256,256]{1,0:T(8,128)} custom-call(s32[2,32,2]{2,1,0:T(8,128)} %get-tuple-element.11.shifts, s32[2,1,32]{2,1,0:T(1,128)} %get-tuple-element.12.weights, bf16[2,2,512,256]{3,2,1,0:T(8,128)(2,1)} %bitcast.2, f32[4,128,128]{2,1,0:T(8,128)} %get-tuple-element.14.masks, bf16[256,256]{1,0:T(8,128)(2,1)} %get-tuple-element.15.row_ref, ...), custom_call_target="tpu_custom_call" | custom-call | tf_op jit(solution)/shard_map/image/pallas_call | solution.py:330
  44.2 9.7 %diffuse.1 = f32[256,256]{1,0:T(8,128)} custom-call(f32[256,256]{1,0:T(8,128)} %image.1.acid_ref), custom_call_target="tpu_custom_call" | custom-call | tf_op jit(solution)/shard_map/diffuse/pallas_call | solution.py:423
  54.0 1.7 %copy.7 = f32[256,256]{1,0:T(8,128)} copy(f32[256,256]{1,0:T(8,128)} %diffuse.1) | data formatting | bytes 524288
Async XLA Ops:
  0.0 0.7 %copy-start = (s32[32,2]{0,1:T(2,128)S(1)}, s32[32,2]{0,1:T(2,128)}, u32[]{:S(2)}) copy-start(s32[32,2]{0,1:T(2,128)} %param.6) | copy-start | bytes 772
